TPU v7x, 32 devices: a whole 2x2x4 slice. The times are simulated.
32 devices in a mesh: prow: 8 (over z, x), pcol: 4 (over y, core).
Axes of the slice: x: 2, y: 2, z: 4, core: 2. Of those that a mesh axis runs over, the one named last changes fastest.
Arguments:
- matrix: float32 [16384, 16384], P('prow', 'pcol'), may hold values from -6 to 6
Outputs:
- reduced: float32 [16384, 16384], P('prow', 'pcol')
- householder_coefficients: float32 [2, 8], replicated
All inputs are finite; a program needn't handle non-finite values.
Results may differ from a plain program's by a relative error of at most 0.0003.
Values sent between devices are 32-bit elements; how exact they have to be, the bound alone decides.
A program may use at most 128 MiB of HBM per device.

v0:
```python
import functools

import jax
import jax.numpy as jnp
from jax import lax
from jax.experimental import pallas as pl
from jax.experimental.pallas import tpu as pltpu
from jax.sharding import PartitionSpec as P

NB = 8
EPS = 1e-06
LANES = 128
YC = 4
XC = 2
MESH = pl.DeviceIdType.MESH


def householder(alpha, sumsq):
    beta = jnp.where(alpha >= 0.0, -1.0, 1.0) * jnp.sqrt(sumsq + EPS)
    return beta, (beta - alpha) / beta, alpha - beta


def lane_sum(x):
    return jnp.sum(x, axis=1, keepdims=True)


def total(x):
    return jnp.sum(lane_sum(x), axis=0, keepdims=True)


def panel_kernel(np_, nq, a_hbm, left_o, right_o, scal_o,
                 a, strip, arows, colp, rowp, v_s, x_s, y_s, u_s, vb, ub,
                 ybuf, xbuf, column_s,
                 a_sem, strip_sem, arow_sem, col_ssem, col_rsem, row_ssem, row_rsem,
                 y_ssem, y_rsem, x_ssem, x_rsem):
    me_p = lax.axis_index("prow")
    me_q = lax.axis_index("pcol")
    rows, cols = a.shape
    rs, cs = rows // LANES, cols // LANES
    chunk = cols // YC
    per = chunk // LANES
    xper = rs // XC

    strip_cp = pltpu.make_async_copy(a_hbm.at[:, pl.ds(0, LANES)], strip, strip_sem)
    strip_cp.start()
    arow_cp = pltpu.make_async_copy(a_hbm.at[pl.ds(0, NB), :], arows, arow_sem)
    arow_cp.start()
    a_cps = []
    for c in range(YC):
        cp = pltpu.make_async_copy(
            a_hbm.at[:, pl.ds(c * chunk, chunk)], a.at[:, pl.ds(c * chunk, chunk)], a_sem.at[c])
        cp.start()
        a_cps.append(cp)

    barrier = pltpu.get_barrier_semaphore()
    for d in range(1, np_):
        pl.semaphore_signal(barrier, inc=1, device_id={"prow": lax.rem(me_p + d, np_)}, device_id_type=MESH)
    for d in range(1, nq):
        pl.semaphore_signal(barrier, inc=1, device_id={"pcol": lax.rem(me_q + d, nq)}, device_id_type=MESH)
    pl.semaphore_wait(barrier, np_ + nq - 2)

    lane8 = lax.broadcasted_iota(jnp.int32, (8, LANES), 1)
    sub8 = lax.broadcasted_iota(jnp.int32, (8, LANES), 0)
    row_gl = (me_p * rows + lax.broadcasted_iota(jnp.int32, (rs, LANES), 0) * LANES
              + lax.broadcasted_iota(jnp.int32, (rs, LANES), 1))
    col_gl = (me_q * cols + lax.broadcasted_iota(jnp.int32, (cs, LANES), 0) * LANES
              + lax.broadcasted_iota(jnp.int32, (cs, LANES), 1))

    strip_cp.wait()
    arow_cp.wait()

    def col_copy(d):
        return pltpu.make_async_remote_copy(
            src_ref=colp, dst_ref=colp, send_sem=col_ssem.at[d], recv_sem=col_rsem,
            device_id={"pcol": lax.rem(me_q + d, nq)}, device_id_type=MESH)

    def row_copy(i, d):
        return pltpu.make_async_remote_copy(
            src_ref=rowp.at[i], dst_ref=rowp.at[i], send_sem=row_ssem.at[i, d], recv_sem=row_rsem.at[i],
            device_id={"prow": lax.rem(me_p + d, np_)}, device_id_type=MESH)

    @pl.when(me_q == 0)
    def _():
        @pl.loop(0, rs)
        def _(s):
            t = strip[pl.ds(s * LANES, LANES), :].T
            for c in range(NB + 1):
                colp[c, pl.ds(s, 1), :] = t[c:c + 1, :]
        for d in range(1, nq):
            col_copy(d).start()

    @pl.when(me_p == 0)
    def _():
        for s in range(cs):
            blk = arows[:, s * LANES:(s + 1) * LANES]
            for i in range(NB):
                rowp[i, s:s + 1, :] = blk[i:i + 1, :]
        for i in range(2):
            for d in range(1, np_):
                row_copy(i, d).start()

    for ref in (v_s, x_s, y_s, u_s):
        ref[...] = jnp.zeros(ref.shape, jnp.float32)

    @pl.when(me_q != 0)
    def _():
        col_copy(1).wait_recv()

    column_s[...] = colp[0]

    def y_copy(i, d, c):
        lo, n = (0, 8 + per) if c == 0 else (8 + c * per, per)
        ref = ybuf.at[i, me_p, pl.ds(lo, n), :]
        return pltpu.make_async_remote_copy(
            src_ref=ref, dst_ref=ref, send_sem=y_ssem.at[d, c], recv_sem=y_rsem.at[lax.rem(i, 2), d, c],
            device_id={"prow": lax.rem(me_p + d, np_)}, device_id_type=MESH)

    def x_copy(i, d, c):
        lo, n = (0, 8 + xper) if c == 0 else (8 + c * xper, xper)
        ref = xbuf.at[i, me_q, pl.ds(lo, n), :]
        return pltpu.make_async_remote_copy(
            src_ref=ref, dst_ref=ref, send_sem=x_ssem.at[d, c], recv_sem=x_rsem.at[lax.rem(i, 2), d, c],
            device_id={"pcol": lax.rem(me_q + d, nq)}, device_id_type=MESH)

    def scalar_tile(first, second, vec, unit):
        tile = jnp.zeros((8, LANES), jnp.float32)
        for k, (ref, w) in enumerate(((first, vec), (second, vec), (first, unit), (second, unit))):
            s = lane_sum(jnp.sum(ref[...] * w[None], axis=1))
            tile = jnp.where(lane8 == k, s, tile)
        s = jnp.where(sub8[:, :1] == 0, total(vec * unit), total(vec * vec))
        return jnp.where(lane8 == 4, s, tile)

    def unpack(tile):
        return [jnp.broadcast_to(lane_sum(jnp.where(lane8 == k, tile, 0.0)), (8, LANES)) for k in range(5)]

    def combine(coef_a, ref_a, coef_b, ref_b):
        acc = coef_a[0:1] * ref_a[0] + coef_b[0:1] * ref_b[0]
        for j in range(1, NB):
            acc = acc + (coef_a[j:j + 1] * ref_a[j] + coef_b[j:j + 1] * ref_b[j])
        return acc

    @pl.loop(0, NB)
    def _(i):
        masked = jnp.where(row_gl >= i, column_s[...], 0.0)
        unit_r = (row_gl == i).astype(jnp.float32)
        column_s[...] = masked

        @pl.loop(0, rs, unroll=min(8, rs))
        def _(s):
            row = jnp.broadcast_to(column_s[pl.ds(s, 1), :], (8, LANES))
            for g in range(LANES // 8):
                col = lane_sum(jnp.where(lane8 == sub8 + 8 * g, row, 0.0))
                vb[pl.ds(s * LANES + 8 * g, 8), :] = jnp.broadcast_to(col, (8, LANES))

        ybuf[i, me_p, 0:8, :] = scalar_tile(v_s, x_s, masked, unit_r)
        for c in range(YC):
            @pl.when(i == 0)
            def _(c=c):
                a_cps[c].wait()

            def body(g, accs):
                accs = list(accs)
                for k in range(8):
                    r = pl.ds(pl.multiple_of(g * 64 + 8 * k, 8), 8)
                    v = vb[r, :]
                    for j in range(per):
                        lo = c * chunk + j * LANES
                        m = (k % 2) * per + j
                        accs[m] = accs[m] + v * a[r, lo:lo + LANES]
                return tuple(accs)

            accs = lax.fori_loop(0, rows // 64, body, (jnp.zeros((8, LANES), jnp.float32),) * (2 * per))
            for j in range(per):
                t = 8 + c * per + j
                ybuf[i, me_p, t:t + 1, :] = jnp.sum(accs[j] + accs[per + j], axis=0, keepdims=True)
            for d in range(1, np_):
                y_copy(i, d, c).start()

        @pl.when(jnp.logical_and(me_p == 0, i < NB - 2))
        def _():
            for d in range(1, np_):
                row_copy(i + 2, d).start()

        @pl.when(me_p != 0)
        def _():
            row_copy(i, 1).wait_recv()

        for c in range(YC):
            for d in range(1, np_):
                y_copy(i, d, c).wait()
        summed = ybuf[i, 0]
        for p in range(1, np_):
            summed = summed + ybuf[i, p]
        v_coef, x_coef, v_at, x_at, misc = unpack(summed[0:8])
        beta, tau, denom = householder(misc[0:1], misc[1:2])
        row_eff = rowp[i] - combine(v_at, y_s, x_at, u_s)
        inv = 1.0 / denom
        trans = (summed[8:] - combine(v_coef, y_s, x_coef, u_s) - beta * row_eff) * inv
        y_new = jnp.where(col_gl > i, tau * trans, 0.0)
        v_s[i] = (masked - beta * unit_r) * inv
        y_s[i] = y_new
        scal_o[0, pl.ds(i, 1), :] = beta
        scal_o[2, pl.ds(i, 1), :] = tau

        row_m = jnp.where(col_gl > i, row_eff - y_new, 0.0)
        unit_c = (col_gl == i + 1).astype(jnp.float32)
        ub[...] = row_m
        xbuf[i, me_q, 0:8, :] = scalar_tile(y_s, u_s, row_m, unit_c)
        for c in range(XC):
            @pl.loop(c * xper, (c + 1) * xper, unroll=min(4, xper))
            def _(s):
                us = [jnp.broadcast_to(ub[j:j + 1, :], (8, LANES)) for j in range(cs)]
                tile = jnp.zeros((8, LANES), jnp.float32)
                for g in range(LANES // 8):
                    r = pl.ds(pl.multiple_of(s * LANES + 8 * g, 8), 8)
                    p0 = us[0] * a[r, 0:LANES]
                    p1 = us[1] * a[r, LANES:2 * LANES]
                    for j in range(2, cs, 2):
                        p0 = p0 + us[j] * a[r, j * LANES:(j + 1) * LANES]
                        p1 = p1 + us[j + 1] * a[r, (j + 1) * LANES:(j + 2) * LANES]
                    tile = jnp.where(lane8 == sub8 + 8 * g, lane_sum(p0 + p1), tile)
                xbuf[i, me_q, pl.ds(8 + s, 1), :] = jnp.sum(tile, axis=0, keepdims=True)
            for d in range(1, nq):
                x_copy(i, d, c).start()
        for c in range(XC):
            for d in range(1, nq):
                x_copy(i, d, c).wait()
        xsum = xbuf[i, 0]
        for q in range(1, nq):
            xsum = xsum + xbuf[i, q]
        y_coef, u_coef, y_at, u_at, misc2 = unpack(xsum[0:8])
        beta2, tau2, denom2 = householder(misc2[0:1], misc2[1:2])
        col_next = colp[i + 1] - combine(y_at, v_s, u_at, x_s)
        inv2 = 1.0 / denom2
        prod = (xsum[8:] - combine(y_coef, v_s, u_coef, x_s) - beta2 * col_next) * inv2
        x_new = jnp.where(row_gl > i, tau2 * prod, 0.0)
        x_s[i] = x_new
        u_s[i] = (row_m - beta2 * unit_c) * inv2
        scal_o[1, pl.ds(i, 1), :] = beta2
        scal_o[3, pl.ds(i, 1), :] = tau2
        column_s[...] = col_next - x_new

    for s in range(rs):
        left_o[0:NB, s * LANES:(s + 1) * LANES] = v_s[:, s, :]
        left_o[NB:, s * LANES:(s + 1) * LANES] = x_s[:, s, :]
    for s in range(cs):
        right_o[0:NB, s * LANES:(s + 1) * LANES] = y_s[:, s, :]
        right_o[NB:, s * LANES:(s + 1) * LANES] = u_s[:, s, :]

    @pl.when(me_q == 0)
    def _():
        for d in range(1, nq):
            col_copy(d).wait_send()

    @pl.when(me_p == 0)
    def _():
        @pl.loop(0, NB)
        def _(i):
            for d in range(1, np_):
                row_copy(i, d).wait_send()


def reduce_panel(matrix, np_, nq):
    rows, cols = matrix.shape
    rs, cs = rows // LANES, cols // LANES
    f32 = jnp.float32
    vmem = pl.BlockSpec(memory_space=pltpu.VMEM)
    dma = pltpu.SemaphoreType.DMA
    return pl.pallas_call(
        functools.partial(panel_kernel, np_, nq),
        out_shape=(jax.ShapeDtypeStruct((2 * NB, rows), f32),
                   jax.ShapeDtypeStruct((2 * NB, cols), f32),
                   jax.ShapeDtypeStruct((4, NB, LANES), f32)),
        in_specs=[pl.BlockSpec(memory_space=pl.ANY)],
        out_specs=(vmem, vmem, vmem),
        scratch_shapes=[
            pltpu.VMEM((rows, cols), f32),
            pltpu.VMEM((rows, LANES), f32),
            pltpu.VMEM((NB, cols), f32),
            pltpu.VMEM((NB + 1, rs, LANES), f32),
            pltpu.VMEM((NB, cs, LANES), f32),
            pltpu.VMEM((NB, rs, LANES), f32),
            pltpu.VMEM((NB, rs, LANES), f32),
            pltpu.VMEM((NB, cs, LANES), f32),
            pltpu.VMEM((NB, cs, LANES), f32),
            pltpu.VMEM((rows, LANES), f32),
            pltpu.VMEM((cs, LANES), f32),
            pltpu.VMEM((NB, np_, 8 + cs, LANES), f32),
            pltpu.VMEM((NB, nq, 8 + rs, LANES), f32),
            pltpu.VMEM((rs, LANES), f32),
            dma((YC,)), dma, dma,
            dma((nq,)), dma, dma((NB, np_)), dma((NB,)),
            dma((np_, YC)), dma((2, np_, YC)), dma((nq, XC)), dma((2, nq, XC)),
        ],
        compiler_params=pltpu.CompilerParams(
            collective_id=0, has_side_effects=True, vmem_limit_bytes=60 * 1024 * 1024),
    )(matrix)


def pieces(x):
    hi = x.astype(jnp.bfloat16)
    rest = x - hi.astype(jnp.float32)
    mid = rest.astype(jnp.bfloat16)
    lo = (rest - mid.astype(jnp.float32)).astype(jnp.bfloat16)
    return hi, mid, lo


def update_kernel(a_ref, left_ref, right_ref, scal_ref, out_ref):
    me_p = lax.axis_index("prow")
    me_q = lax.axis_index("pcol")
    step = pl.program_id(0)
    block, cols = a_ref.shape
    lh, lm, ll = pieces(left_ref[...])
    rh, rm, rl = pieces(right_ref[...])
    left = jnp.concatenate([lh, lh, lh, lm, lm, ll], axis=0)
    right = jnp.concatenate([rh, rm, rl, rh, rm, rh], axis=0)
    dims = (((0,), (0,)), ((), ()))
    out_ref[...] = a_ref[...] - lax.dot_general(left, right, dims, preferred_element_type=jnp.float32)

    k = left.shape[0]
    src = lax.broadcasted_iota(jnp.int32, (k, LANES), 0)
    lane = lax.broadcasted_iota(jnp.int32, (k, LANES), 1)
    pick = jnp.logical_and(
        lane < NB, (src == lane) | (src == lane + 6 * NB) | (src == lane + 10 * NB))
    vt = lax.dot_general(left, jnp.where(pick, 1.0, 0.0).astype(jnp.bfloat16), dims,
                         preferred_element_type=jnp.float32)

    @pl.when(me_q == 0)
    def _():
        lanes = lax.broadcasted_iota(jnp.int32, (block, LANES), 1)
        out_ref[:, 0:LANES] = jnp.where(lanes < NB, vt, out_ref[:, 0:LANES])

    @pl.when(jnp.logical_and(me_p == 0, step == 0))
    def _():
        out_ref[0:NB, :] = right_ref[NB:, :]

        @pl.when(me_q == 0)
        def _():
            r = lax.broadcasted_iota(jnp.int32, (NB, LANES), 0)
            c = lax.broadcasted_iota(jnp.int32, (NB, LANES), 1)
            out_ref[0:NB, 0:LANES] = jnp.where(
                c < r, vt[0:NB, :],
                jnp.where(c == r, scal_ref[0], jnp.where(c == r + 1, scal_ref[1], right_ref[NB:, 0:LANES])))


def apply_panel(matrix, left, right, scal):
    rows, cols = matrix.shape
    block = min(rows, 256)
    return pl.pallas_call(
        update_kernel,
        out_shape=jax.ShapeDtypeStruct((rows, cols), jnp.float32),
        grid=(rows // block,),
        in_specs=[
            pl.BlockSpec((block, cols), lambda i: (i, 0)),
            pl.BlockSpec((2 * NB, block), lambda i: (0, i)),
            pl.BlockSpec((2 * NB, cols), lambda i: (0, 0)),
            pl.BlockSpec((4, NB, LANES), lambda i: (0, 0, 0)),
        ],
        out_specs=pl.BlockSpec((block, cols), lambda i: (i, 0)),
        compiler_params=pltpu.CompilerParams(vmem_limit_bytes=48 * 1024 * 1024),
    )(matrix, left, right, scal)


def solution(mesh):
    np_, nq = mesh.shape["prow"], mesh.shape["pcol"]

    def per_device(matrix):
        left, right, scal = reduce_panel(matrix, np_, nq)
        return apply_panel(matrix, left, right, scal), scal[2:4, :, 0]

    return jax.shard_map(
        per_device, mesh=mesh, in_specs=(P("prow", "pcol"),),
        out_specs=(P("prow", "pcol"), P()), check_vma=False)
```

profile of v0, /device:TPU:0, one launch (start us, length us, event | category | flops | bytes accessed | tf_op | source)
XLA Modules:
  0.0 152.0 jit_solution(9713773125473408838)
XLA Ops:
  0.6 124.0 %shard_map.30 = (f32[16,2048]{1,0:T(8,128)}, f32[16,4096]{1,0:T(8,128)}, f32[4,8,128]{2,1,0:T(8,128)}) custom-call(f32[2048,4096]{1,0:T(8,128)} %a_ref.1), custom_call_target="tpu_custom_call" | custom-call | tf_op jit(solution)/shard_map/pallas_call | solution.py:269
  124.6 0.0 copy-start
  124.6 0.9 copy-done
  125.6 0.0 copy-start.1
  125.6 0.9 copy-done.1
  126.5 0.0 copy-start.2
  126.5 0.7 copy-done.2
  127.2 24.2 %shard_map.31 = f32[2048,4096]{1,0:T(8,128)} custom-call(f32[2048,4096]{1,0:T(8,128)} %a_ref.1, f32[16,2048]{1,0:T(8,128)S(1)} %copy-done.1, f32[16,4096]{1,0:T(8,128)S(1)} %copy-done, f32[4,8,128]{2,1,0:T(8,128)S(1)} %copy-done.2), custom_call_target="tpu_custom_call" | custom-call | tf_op jit(solution)/shard_map/pallas_call | solution.py:349
  151.4 0.6 slice_reduce_fusion
Async XLA Ops:
  124.6 1.0 copy-start
  125.6 0.9 copy-start.1
  126.5 0.7 copy-start.2
where the time goes:
time: 152 us
  Pallas kernels  148 us (97%)
  local copies, waits for them, and re-layouts  3.21 us (2%)
    pallas_call x1, Pallas kernels, reduce_panel(): pl.pallas_call(functools.partial(panel_kernel, np_, nq), out_shape=(jax.S...  124 us
    pallas_call x1, Pallas kernels, apply_panel(): pl.pallas_call(update_kernel, out_shape=jax.ShapeDtypeStruct((rows, cols)...  24.2 us

commit v1 on v0

v1 whole, which is shorter than its diff:
```python
import functools

import jax
import jax.numpy as jnp
from jax import lax
from jax.experimental import pallas as pl
from jax.experimental.pallas import tpu as pltpu
from jax.sharding import PartitionSpec as P

NB = 8
EPS = 1e-06
LANES = 128
Y_PARTS = (1, 2, 3, 2)
XC = 2
UPDATE_ROWS = 128
MESH = pl.DeviceIdType.MESH


def householder(alpha, sumsq):
    beta = jnp.where(alpha >= 0.0, -1.0, 1.0) * jnp.sqrt(sumsq + EPS)
    return beta, (beta - alpha) / beta, alpha - beta


def lane_sum(x):
    return jnp.sum(x, axis=1, keepdims=True)


def total(x):
    return jnp.sum(lane_sum(x), axis=0, keepdims=True)


def y_chunks(cs):
    unit = cs // sum(Y_PARTS)
    sizes = [unit * part for part in Y_PARTS]
    return [(sum(sizes[:c]), n) for c, n in enumerate(sizes)]


def peers(me, n):
    if n & (n - 1):
        return [(d, lax.rem(me + d, n)) for d in range(1, n)]
    out = []
    for m in range(n - 1, 0, -1):
        other = me
        for b in range(n.bit_length() - 1):
            if m >> b & 1:
                other = other + (1 - 2 * lax.rem(me // (1 << b), 2)) * (1 << b)
        out.append((m, other))
    return out


def panel_kernel(np_, nq, a_hbm, a, left_o, right_o, scal_o,
                 strip, arows, colp, rowp, v_s, x_s, y_s, u_s, vb, ub, acc_s,
                 ybuf, xbuf, column_s,
                 a_sem, strip_sem, arow_sem, col_ssem, col_rsem, row_ssem, row_rsem,
                 y_ssem, y_rsem, x_ssem, x_rsem):
    me_p = lax.axis_index("prow")
    me_q = lax.axis_index("pcol")
    rows, cols = a.shape
    rs, cs = rows // LANES, cols // LANES
    ych = y_chunks(cs)
    xper = rs // XC
    groups = LANES // 8
    p_peers, q_peers = peers(me_p, np_), peers(me_q, nq)

    strip_cp = pltpu.make_async_copy(a_hbm.at[:, pl.ds(0, LANES)], strip, strip_sem)
    strip_cp.start()
    arow_cp = pltpu.make_async_copy(a_hbm.at[pl.ds(0, NB), :], arows, arow_sem)
    arow_cp.start()
    a_cps = []
    for c, (lo, n) in enumerate(ych):
        part = pl.ds(lo * LANES, n * LANES)
        cp = pltpu.make_async_copy(a_hbm.at[:, part], a.at[:, part], a_sem.at[c])
        cp.start()
        a_cps.append(cp)

    barrier = pltpu.get_barrier_semaphore()
    for d in range(1, np_):
        pl.semaphore_signal(barrier, inc=1, device_id={"prow": lax.rem(me_p + d, np_)}, device_id_type=MESH)
    for d in range(1, nq):
        pl.semaphore_signal(barrier, inc=1, device_id={"pcol": lax.rem(me_q + d, nq)}, device_id_type=MESH)
    pl.semaphore_wait(barrier, np_ + nq - 2)

    lane8 = lax.broadcasted_iota(jnp.int32, (8, LANES), 1)
    sub8 = lax.broadcasted_iota(jnp.int32, (8, LANES), 0)
    row_gl = (me_p * rows + lax.broadcasted_iota(jnp.int32, (rs, LANES), 0) * LANES
              + lax.broadcasted_iota(jnp.int32, (rs, LANES), 1))

    def col_gl(lo, n):
        return (me_q * cols + (lo + lax.broadcasted_iota(jnp.int32, (n, LANES), 0)) * LANES
                + lax.broadcasted_iota(jnp.int32, (n, LANES), 1))

    strip_cp.wait()
    arow_cp.wait()

    def col_copy(d):
        return pltpu.make_async_remote_copy(
            src_ref=colp, dst_ref=colp, send_sem=col_ssem.at[d], recv_sem=col_rsem,
            device_id={"pcol": lax.rem(me_q + d, nq)}, device_id_type=MESH)

    def row_copy(i, d):
        return pltpu.make_async_remote_copy(
            src_ref=rowp.at[i], dst_ref=rowp.at[i], send_sem=row_ssem.at[i, d], recv_sem=row_rsem.at[i],
            device_id={"prow": lax.rem(me_p + d, np_)}, device_id_type=MESH)

    @pl.when(me_q == 0)
    def _():
        @pl.loop(0, rs)
        def _(s):
            t = strip[pl.ds(s * LANES, LANES), :].T
            for c in range(NB + 1):
                colp[c, pl.ds(s, 1), :] = t[c:c + 1, :]
        for d in range(1, nq):
            col_copy(d).start()

    @pl.when(me_p == 0)
    def _():
        for s in range(cs):
            blk = arows[:, s * LANES:(s + 1) * LANES]
            for i in range(NB):
                rowp[i, s:s + 1, :] = blk[i:i + 1, :]
        for i in range(2):
            for d in range(1, np_):
                row_copy(i, d).start()

    for ref in (v_s, x_s, y_s, u_s):
        ref[...] = jnp.zeros(ref.shape, jnp.float32)

    @pl.when(me_q != 0)
    def _():
        col_copy(1).wait_recv()

    column_s[...] = colp[0]

    def y_copy(i, m, peer, c):
        lo, n = ych[c]
        lo, n = (0, 8 + n) if c == 0 else (8 + lo, n)
        ref = ybuf.at[i, me_p, pl.ds(lo, n), :]
        return pltpu.make_async_remote_copy(
            src_ref=ref, dst_ref=ref, send_sem=y_ssem.at[m, c], recv_sem=y_rsem.at[lax.rem(i, 2), m, c],
            device_id={"prow": peer}, device_id_type=MESH)

    def x_copy(i, m, peer, c):
        lo, n = (0, 8 + xper) if c == 0 else (8 + c * xper, xper)
        ref = xbuf.at[i, me_q, pl.ds(lo, n), :]
        return pltpu.make_async_remote_copy(
            src_ref=ref, dst_ref=ref, send_sem=x_ssem.at[m, c], recv_sem=x_rsem.at[lax.rem(i, 2), m, c],
            device_id={"pcol": peer}, device_id_type=MESH)

    def scalar_tile(first, second, vec, here, at):
        tile = jnp.zeros((8, LANES), jnp.float32)
        for k, ref in enumerate((first, second)):
            tile = jnp.where(lane8 == k, lane_sum(jnp.sum(ref[...] * vec[None], axis=1)), tile)
        hit = jnp.logical_and(here, lane8 == at)
        for k, ref in enumerate((first, second)):
            tile = jnp.where(lane8 == 2 + k, lane_sum(jnp.where(hit, ref[:, 0, :], 0.0)), tile)
        alpha = lane_sum(jnp.where(hit[0:1], vec[0:1], 0.0))
        s = jnp.where(sub8[:, :1] == 0, alpha, total(vec * vec))
        return jnp.where(lane8 == 4, s, tile)

    def unpack(tile):
        return [jnp.broadcast_to(lane_sum(jnp.where(lane8 == k, tile, 0.0)), (8, LANES)) for k in range(5)]

    def combine(coef_a, ref_a, coef_b, ref_b, lo, n):
        part = pl.ds(lo, n)
        acc = coef_a[0:1] * ref_a[0, part, :] + coef_b[0:1] * ref_b[0, part, :]
        for j in range(1, NB):
            acc = acc + (coef_a[j:j + 1] * ref_a[j, part, :] + coef_b[j:j + 1] * ref_b[j, part, :])
        return acc

    def spread(s):
        row = jnp.broadcast_to(column_s[s:s + 1, :], (8, LANES))
        return [jnp.broadcast_to(lane_sum(jnp.where(lane8 == sub8 + 8 * g, row, 0.0)), (8, LANES))
                for g in range(groups)]

    def y_finish(i, c, accs):
        lo, n = ych[c]
        for j in range(n):
            t = 8 + lo + j
            ybuf[i, me_p, t:t + 1, :] = jnp.sum(accs[j] + accs[n + j], axis=0, keepdims=True)
        for m, peer in p_peers:
            y_copy(i, m, peer, c).start()

    @pl.loop(0, NB)
    def _(i):
        masked = jnp.where(row_gl >= i, column_s[...], 0.0)
        unit_r = (row_gl == i).astype(jnp.float32)
        column_s[...] = masked
        ybuf[i, me_p, 0:8, :] = scalar_tile(v_s, x_s, masked, me_p == 0, i)

        for c, (lo, n) in enumerate(ych):
            @pl.when(i == 0)
            def _(c=c):
                a_cps[c].wait()

            if c == 0:
                accs = [jnp.zeros((8, LANES), jnp.float32)] * (2 * n)
                for s in range(rs):
                    for g, v in enumerate(spread(s)):
                        r = pl.ds(s * LANES + 8 * g, 8)
                        vb[r, :] = v
                        for j in range(n):
                            m = (g % 2) * n + j
                            accs[m] = accs[m] + v * a[r, (lo + j) * LANES:(lo + j + 1) * LANES]
            else:
                def body(s, accs, lo=lo, n=n):
                    accs = list(accs)
                    for g in range(groups):
                        r = pl.ds(pl.multiple_of(s * LANES + 8 * g, 8), 8)
                        v = vb[r, :]
                        for j in range(n):
                            m = (g % 2) * n + j
                            accs[m] = accs[m] + v * a[r, (lo + j) * LANES:(lo + j + 1) * LANES]
                    return tuple(accs)

                accs = lax.fori_loop(0, rs, body, (jnp.zeros((8, LANES), jnp.float32),) * (2 * n))
            y_finish(i, c, accs)

        @pl.when(jnp.logical_and(me_p == 0, i < NB - 2))
        def _():
            for d in range(1, np_):
                row_copy(i + 2, d).start()

        @pl.when(me_p != 0)
        def _():
            row_copy(i, 1).wait_recv()

        for c, (lo, n) in enumerate(ych):
            for m, peer in p_peers:
                y_copy(i, m, peer, c).wait_recv()
            if c == 0:
                tile = ybuf[i, 0, 0:8, :]
                for p in range(1, np_):
                    tile = tile + ybuf[i, p, 0:8, :]
                v_coef, x_coef, v_at, x_at, misc = unpack(tile)
                beta, tau, denom = householder(misc[0:1], misc[1:2])
                inv = 1.0 / denom
                v_s[i] = (masked - beta * unit_r) * inv
                scal_o[0, pl.ds(i, 1), :] = beta
                scal_o[2, pl.ds(i, 1), :] = tau
            part, buf = pl.ds(lo, n), pl.ds(8 + lo, n)
            summed = ybuf[i, 0, buf, :]
            for p in range(1, np_):
                summed = summed + ybuf[i, p, buf, :]
            row_eff = rowp[i, part, :] - combine(v_at, y_s, x_at, u_s, lo, n)
            trans = (summed - combine(v_coef, y_s, x_coef, u_s, lo, n) - beta * row_eff) * inv
            mine = col_gl(lo, n) > i
            y_new = jnp.where(mine, tau * trans, 0.0)
            y_s[i, part, :] = y_new
            ub[part, :] = jnp.where(mine, row_eff - y_new, 0.0)
            us = [jnp.broadcast_to(ub[lo + j:lo + j + 1, :], (8, LANES)) for j in range(n)]

            def product(r, us=us, lo=lo, n=n):
                p = [us[k] * a[r, (lo + k) * LANES:(lo + k + 1) * LANES] for k in range(2)]
                for j in range(2, n):
                    p[j % 2] = p[j % 2] + us[j] * a[r, (lo + j) * LANES:(lo + j + 1) * LANES]
                return p[0] + p[1]

            if c < len(ych) - 1:
                @pl.loop(0, rs)
                def _(s, c=c, product=product):
                    for g in range(groups):
                        r = pl.ds(pl.multiple_of(s * LANES + 8 * g, 8), 8)
                        acc_s[r, :] = product(r) if c == 0 else acc_s[r, :] + product(r)
            else:
                row_m = ub[...]
                xbuf[i, me_q, 0:8, :] = scalar_tile(y_s, u_s, row_m, me_q == 0, i + 1)
                for h in range(XC):
                    @pl.loop(h * xper, (h + 1) * xper, unroll=min(4, xper))
                    def _(s, product=product):
                        tile = jnp.zeros((8, LANES), jnp.float32)
                        for g in range(groups):
                            r = pl.ds(pl.multiple_of(s * LANES + 8 * g, 8), 8)
                            tile = jnp.where(lane8 == sub8 + 8 * g, lane_sum(acc_s[r, :] + product(r)), tile)
                        xbuf[i, me_q, pl.ds(8 + s, 1), :] = jnp.sum(tile, axis=0, keepdims=True)
                    for m, peer in q_peers:
                        x_copy(i, m, peer, h).start()

        for c in range(len(ych)):
            for m, peer in p_peers:
                y_copy(i, m, peer, c).wait_send()
        unit_c = (col_gl(0, cs) == i + 1).astype(jnp.float32)
        for h in range(XC):
            for m, peer in q_peers:
                x_copy(i, m, peer, h).wait()
        xsum = xbuf[i, 0]
        for q in range(1, nq):
            xsum = xsum + xbuf[i, q]
        y_coef, u_coef, y_at, u_at, misc2 = unpack(xsum[0:8])
        beta2, tau2, denom2 = householder(misc2[0:1], misc2[1:2])
        col_next = colp[i + 1] - combine(y_at, v_s, u_at, x_s, 0, rs)
        inv2 = 1.0 / denom2
        prod = (xsum[8:] - combine(y_coef, v_s, u_coef, x_s, 0, rs) - beta2 * col_next) * inv2
        x_new = jnp.where(row_gl > i, tau2 * prod, 0.0)
        x_s[i] = x_new
        u_s[i] = (row_m - beta2 * unit_c) * inv2
        scal_o[1, pl.ds(i, 1), :] = beta2
        scal_o[3, pl.ds(i, 1), :] = tau2
        column_s[...] = col_next - x_new

    for s in range(rs):
        left_o[0:NB, s * LANES:(s + 1) * LANES] = v_s[:, s, :]
        left_o[NB:, s * LANES:(s + 1) * LANES] = x_s[:, s, :]
    for s in range(cs):
        right_o[0:NB, s * LANES:(s + 1) * LANES] = y_s[:, s, :]
        right_o[NB:, s * LANES:(s + 1) * LANES] = u_s[:, s, :]

    @pl.when(me_q == 0)
    def _():
        for d in range(1, nq):
            col_copy(d).wait_send()

    @pl.when(me_p == 0)
    def _():
        @pl.loop(0, NB)
        def _(i):
            for d in range(1, np_):
                row_copy(i, d).wait_send()


def reduce_panel(matrix, np_, nq):
    rows, cols = matrix.shape
    rs, cs = rows // LANES, cols // LANES
    f32 = jnp.float32
    vmem = pl.BlockSpec(memory_space=pltpu.VMEM)
    dma = pltpu.SemaphoreType.DMA
    yc = len(Y_PARTS)
    return pl.pallas_call(
        functools.partial(panel_kernel, np_, nq),
        out_shape=(pltpu.VMEM((rows, cols), f32),
                   pltpu.VMEM((2 * NB, rows), f32),
                   pltpu.VMEM((2 * NB, cols), f32),
                   pltpu.VMEM((4, NB, LANES), f32)),
        in_specs=[pl.BlockSpec(memory_space=pl.ANY)],
        out_specs=(vmem, vmem, vmem, vmem),
        scratch_shapes=[
            pltpu.VMEM((rows, LANES), f32),
            pltpu.VMEM((NB, cols), f32),
            pltpu.VMEM((NB + 1, rs, LANES), f32),
            pltpu.VMEM((NB, cs, LANES), f32),
            pltpu.VMEM((NB, rs, LANES), f32),
            pltpu.VMEM((NB, rs, LANES), f32),
            pltpu.VMEM((NB, cs, LANES), f32),
            pltpu.VMEM((NB, cs, LANES), f32),
            pltpu.VMEM((rows, LANES), f32),
            pltpu.VMEM((cs, LANES), f32),
            pltpu.VMEM((rows, LANES), f32),
            pltpu.VMEM((NB, np_, 8 + cs, LANES), f32),
            pltpu.VMEM((NB, nq, 8 + rs, LANES), f32),
            pltpu.VMEM((rs, LANES), f32),
            dma((yc,)), dma, dma,
            dma((nq,)), dma, dma((NB, np_)), dma((NB,)),
            dma((np_, yc)), dma((2, np_, yc)), dma((nq, XC)), dma((2, nq, XC)),
        ],
        compiler_params=pltpu.CompilerParams(
            collective_id=0, has_side_effects=True, vmem_limit_bytes=20 * 1024 * 1024),
    )(matrix)


def pieces(x):
    hi = x.astype(jnp.bfloat16)
    rest = x - hi.astype(jnp.float32)
    mid = rest.astype(jnp.bfloat16)
    lo = (rest - mid.astype(jnp.float32)).astype(jnp.bfloat16)
    return hi, mid, lo


def update_kernel(a_ref, left_ref, right_ref, scal_ref, out_ref, coef_ref, left_p, right_p):
    me_p = lax.axis_index("prow")
    me_q = lax.axis_index("pcol")
    step = pl.program_id(0)
    block, cols = out_ref.shape
    dims = (((0,), (0,)), ((), ()))

    @pl.when(step == 0)
    def _():
        lh, lm, ll = pieces(left_ref[...])
        rh, rm, rl = pieces(right_ref[...])
        for k, (lp, rp) in enumerate(((lh, rh), (lh, rm), (lh, rl), (lm, rh), (lm, rm), (ll, rh))):
            left_p[2 * NB * k:2 * NB * (k + 1), :] = lp
            right_p[2 * NB * k:2 * NB * (k + 1), :] = rp
        lane = lax.broadcasted_iota(jnp.int32, (NB, LANES), 1)
        sub = lax.broadcasted_iota(jnp.int32, (NB, LANES), 0)
        for t in range(2):
            row = jnp.sum(jnp.where(lane == sub, scal_ref[2 + t], 0.0), axis=0, keepdims=True)
            coef_ref[t:t + 1, :] = row[:, 0:NB]

    left = left_p[:, pl.ds(pl.multiple_of(step * block, block), block)]
    rows = pl.ds(pl.multiple_of(step * block, block), block)
    out_ref[...] = a_ref[rows, :] - lax.dot_general(
        left, right_p[...], dims, preferred_element_type=jnp.float32)

    @pl.when(me_q == 0)
    def _():
        k = left.shape[0]
        src = lax.broadcasted_iota(jnp.int32, (k, LANES), 0)
        lane = lax.broadcasted_iota(jnp.int32, (k, LANES), 1)
        pick = jnp.logical_and(
            lane < NB, (src == lane) | (src == lane + 6 * NB) | (src == lane + 10 * NB))
        vt = lax.dot_general(left, jnp.where(pick, 1.0, 0.0).astype(jnp.bfloat16), dims,
                             preferred_element_type=jnp.float32)
        lanes = lax.broadcasted_iota(jnp.int32, (block, LANES), 1)
        out_ref[:, 0:LANES] = jnp.where(lanes < NB, vt, out_ref[:, 0:LANES])

    @pl.when(jnp.logical_and(me_p == 0, step == 0))
    def _():
        vt = out_ref[0:NB, 0:LANES]
        out_ref[0:NB, :] = right_ref[NB:, :]

        @pl.when(me_q == 0)
        def _():
            r = lax.broadcasted_iota(jnp.int32, (NB, LANES), 0)
            c = lax.broadcasted_iota(jnp.int32, (NB, LANES), 1)
            out_ref[0:NB, 0:LANES] = jnp.where(
                c < r, vt,
                jnp.where(c == r, scal_ref[0], jnp.where(c == r + 1, scal_ref[1], right_ref[NB:, 0:LANES])))


def apply_panel(matrix, left, right, scal):
    rows, cols = matrix.shape
    block = min(rows, UPDATE_ROWS)
    vmem = pl.BlockSpec(memory_space=pltpu.VMEM)
    return pl.pallas_call(
        update_kernel,
        out_shape=(jax.ShapeDtypeStruct((rows, cols), jnp.float32),
                   jax.ShapeDtypeStruct((2, NB), jnp.float32)),
        grid=(rows // block,),
        in_specs=[vmem, vmem, vmem, vmem],
        out_specs=(pl.BlockSpec((block, cols), lambda i: (i, 0)),
                   pl.BlockSpec((2, NB), lambda i: (0, 0))),
        scratch_shapes=[pltpu.VMEM((12 * NB, rows), jnp.bfloat16),
                        pltpu.VMEM((12 * NB, cols), jnp.bfloat16)],
        compiler_params=pltpu.CompilerParams(vmem_limit_bytes=20 * 1024 * 1024),
    )(matrix, left, right, scal)


def solution(mesh):
    np_, nq = mesh.shape["prow"], mesh.shape["pcol"]

    def per_device(matrix):
        return apply_panel(*reduce_panel(matrix, np_, nq))

    return jax.shard_map(
        per_device, mesh=mesh, in_specs=(P("prow", "pcol"),),
        out_specs=(P("prow", "pcol"), P()), check_vma=False)
```

time: 152 us -> 123 us (0.81)
  Pallas kernels: 148 us -> 122 us
  local copies, waits for them, and re-layouts: 3.21 us -> 0 us
    pallas_call x2, Pallas kernels: 148 us -> 122 us  [the longest x1 106 us: reduce_panel(): pl.pallas_call(functools.partial(panel_kernel, np_, nq), out_shape=(pltpu...]
    unnamed x6 -> x0, local copies, waits for them, and re-layouts: 2.56 us -> none
where the time goes in v1:
time: 123 us
  Pallas kernels  122 us (99%)
    pallas_call x1, Pallas kernels, reduce_panel(): pl.pallas_call(functools.partial(panel_kernel, np_, nq), out_shape=(pltpu...  106 us
    pallas_call x1, Pallas kernels, apply_panel(): pl.pallas_call(update_kernel, out_shape=(jax.ShapeDtypeStruct((rows, cols...  16.2 us

profile of v1, /device:TPU:0, one launch (start us, length us, event | category | flops | bytes accessed | tf_op | source)
XLA Modules:
  0.0 122.9 jit_solution(18111979015094825447)
XLA Ops:
  0.6 106.1 %shard_map.30 = (f32[2048,4096]{1,0:T(8,128)S(1)}, f32[16,2048]{1,0:T(8,128)S(1)}, f32[16,4096]{1,0:T(8,128)S(1)}, f32[4,8,128]{2,1,0:T(8,128)S(1)}) custom-call(f32[2048,4096]{1,0:T(8,128)} %a_hbm.1), custom_call_target="tpu_custom_call" | custom-call | tf_op jit(solution)/shard_map/pallas_call | solution.py:327
  106.7 16.2 %shard_map.31 = (f32[2048,4096]{1,0:T(8,128)}, f32[2,8]{1,0:T(2,128)}) custom-call(f32[2048,4096]{1,0:T(8,128)S(1)} %get-tuple-element.6.a_ref, f32[16,2048]{1,0:T(8,128)S(1)} %get-tuple-element.7.left_ref, f32[16,4096]{1,0:T(8,128)S(1)} %get-tuple-element.8.right_ref, f32[4,8,128]{2,1,0:T(8,128)S(1)} %get-tuple-element.9.scal_ref), custom_call_target="tpu_custom_call" | custom-call | tf_op jit(solution)/shard_map/pallas_call | solution.py:422

commit v2 on v1

v2 whole, which is shorter than its diff:
```python
import functools

import jax
import jax.numpy as jnp
from jax import lax
from jax.experimental import pallas as pl
from jax.experimental.pallas import tpu as pltpu
from jax.sharding import PartitionSpec as P

NB = 8
EPS = 1e-06
LANES = 128
Y_PARTS = (1, 2, 2, 2, 1)
UPDATE_ROWS = 128
UPDATE_SLOTS = 6
BLOCKS = 2
MESH = pl.DeviceIdType.MESH


def householder(alpha, sumsq):
    beta = jnp.where(alpha >= 0.0, -1.0, 1.0) * jnp.sqrt(sumsq + EPS)
    return beta, (beta - alpha) / beta, alpha - beta


def lane_sum(x):
    return jnp.sum(x, axis=1, keepdims=True)


def total(x):
    return jnp.sum(lane_sum(x), axis=0, keepdims=True)


def y_chunks(cs):
    unit = cs // sum(Y_PARTS)
    sizes = [unit * part for part in Y_PARTS]
    return [(sum(sizes[:c]), n) for c, n in enumerate(sizes)]


def peers(me, n):
    if n & (n - 1):
        return [(d, lax.rem(me + d, n)) for d in range(1, n)]
    out = []
    for m in range(n - 1, 0, -1):
        other = me
        for b in range(n.bit_length() - 1):
            if m >> b & 1:
                other = other + (1 - 2 * lax.rem(me // (1 << b), 2)) * (1 << b)
        out.append((m, other))
    return out


def panel_kernel(np_, nq, a_hbm, a, left_o, right_o, scal_o,
                 strip, arows, colp, rowp, v_s, x_s, y_s, u_s, vb, ub, acc_s,
                 ybuf, xbuf, column_s,
                 a_sem, strip_sem, arow_sem, col_ssem, col_rsem, row_ssem, row_rsem,
                 y_ssem, y_rsem, x_ssem, x_rsem):
    me_p = lax.axis_index("prow")
    me_q = lax.axis_index("pcol")
    rows, cols = a.shape
    rs, cs = rows // LANES, cols // LANES
    ych = y_chunks(cs)
    groups = LANES // 8
    p_peers, q_peers = peers(me_p, np_), peers(me_q, nq)

    strip_cp = pltpu.make_async_copy(a_hbm.at[:, pl.ds(0, LANES)], strip, strip_sem)
    strip_cp.start()
    arow_cp = pltpu.make_async_copy(a_hbm.at[pl.ds(0, NB), :], arows, arow_sem)
    arow_cp.start()
    a_cps = []
    for c, (lo, n) in enumerate(ych):
        part = pl.ds(lo * LANES, n * LANES)
        a_cps.append(pltpu.make_async_copy(a_hbm.at[:, part], a.at[:, part], a_sem.at[c]))
    for cp in a_cps[:2]:
        cp.start()

    barrier = pltpu.get_barrier_semaphore()
    for d in range(1, np_):
        pl.semaphore_signal(barrier, inc=1, device_id={"prow": lax.rem(me_p + d, np_)}, device_id_type=MESH)
    for d in range(1, nq):
        pl.semaphore_signal(barrier, inc=1, device_id={"pcol": lax.rem(me_q + d, nq)}, device_id_type=MESH)
    pl.semaphore_wait(barrier, np_ + nq - 2)

    lane8 = lax.broadcasted_iota(jnp.int32, (8, LANES), 1)
    sub8 = lax.broadcasted_iota(jnp.int32, (8, LANES), 0)
    row_gl = (me_p * rows + lax.broadcasted_iota(jnp.int32, (rs, LANES), 0) * LANES
              + lax.broadcasted_iota(jnp.int32, (rs, LANES), 1))

    def col_gl(lo, n):
        return (me_q * cols + (lo + lax.broadcasted_iota(jnp.int32, (n, LANES), 0)) * LANES
                + lax.broadcasted_iota(jnp.int32, (n, LANES), 1))

    def col_copy(h, d):
        part = colp.at[pl.ds(0, 1)] if h == 0 else colp.at[pl.ds(1, NB)]
        return pltpu.make_async_remote_copy(
            src_ref=part, dst_ref=part, send_sem=col_ssem.at[h, d], recv_sem=col_rsem.at[h],
            device_id={"pcol": lax.rem(me_q + d, nq)}, device_id_type=MESH)

    def row_copy(i, d):
        return pltpu.make_async_remote_copy(
            src_ref=rowp.at[i], dst_ref=rowp.at[i], send_sem=row_ssem.at[i, d], recv_sem=row_rsem.at[i],
            device_id={"prow": lax.rem(me_p + d, np_)}, device_id_type=MESH)

    strip_cp.wait()

    @pl.when(me_q == 0)
    def _():
        @pl.loop(0, rs, unroll=min(8, rs))
        def _(s):
            t = strip[pl.ds(s * LANES, LANES), :].T
            for c in range(NB + 1):
                colp[c, pl.ds(s, 1), :] = t[c:c + 1, :]
        for h in range(2):
            for d in range(1, nq):
                col_copy(h, d).start()

    arow_cp.wait()

    @pl.when(me_p == 0)
    def _():
        for s in range(cs):
            blk = arows[:, s * LANES:(s + 1) * LANES]
            for i in range(NB):
                rowp[i, s:s + 1, :] = blk[i:i + 1, :]
        for i in range(2):
            for d in range(1, np_):
                row_copy(i, d).start()

    for cp in a_cps[2:]:
        cp.start()

    for ref in (v_s, x_s, y_s, u_s, left_o, right_o):
        ref[...] = jnp.zeros(ref.shape, jnp.float32)

    @pl.when(me_q != 0)
    def _():
        col_copy(0, 1).wait_recv()

    column_s[...] = colp[0]

    def y_part(c):
        lo, n = ych[c]
        return pl.ds(7, 1 + n) if c == 0 else pl.ds(8 + lo, n)

    def y_send(i, c):
        ref = ybuf.at[i, me_p, y_part(c), :]
        for m, peer in p_peers:
            pltpu.make_async_remote_copy(
                src_ref=ref, dst_ref=ref, send_sem=y_ssem.at[c], recv_sem=y_rsem.at[lax.rem(i, 2), c],
                device_id={"prow": peer}, device_id_type=MESH).start()

    def y_wait(i, c, sem):
        ref = ybuf.at[i, pl.ds(0, np_ - 1), y_part(c), :]
        pltpu.make_async_copy(ref, ref, sem).wait()

    def x_send(i):
        ref = xbuf.at[i, me_q, pl.ds(7, 1 + rs), :]
        for m, peer in q_peers:
            pltpu.make_async_remote_copy(
                src_ref=ref, dst_ref=ref, send_sem=x_ssem, recv_sem=x_rsem.at[lax.rem(i, 2)],
                device_id={"pcol": peer}, device_id_type=MESH).start()

    def x_wait(i, sem):
        ref = xbuf.at[i, pl.ds(0, nq - 1), pl.ds(7, 1 + rs), :]
        pltpu.make_async_copy(ref, ref, sem).wait()

    def scalar_row(first, second, vec, here, at):
        sums = [lane_sum(jnp.sum(ref[...] * vec[None], axis=1)) for ref in (first, second)]
        hit = jnp.logical_and(here, lane8 == at)
        sums += [lane_sum(jnp.where(hit, ref[:, 0, :], 0.0)) for ref in (first, second)]
        alpha = lane_sum(jnp.where(hit[0:1], vec[0:1], 0.0))
        sums.append(jnp.where(sub8[:, :1] == 0, alpha, total(vec * vec)))
        tile = jnp.zeros((8, LANES), jnp.float32)
        for k, one in enumerate(sums):
            tile = jnp.where(lane8 == sub8 + 8 * k, one, tile)
        return jnp.sum(tile, axis=0, keepdims=True)

    def unpack(buf, n):
        row = buf[0, 7:8, :]
        for p in range(1, n):
            row = row + buf[p, 7:8, :]
        row = jnp.broadcast_to(row, (8, LANES))
        return [jnp.broadcast_to(lane_sum(jnp.where(lane8 == sub8 + 8 * k, row, 0.0)), (8, LANES))
                for k in range(5)]

    def combine(coef_a, ref_a, coef_b, ref_b, lo, n):
        part = pl.ds(lo, n)
        acc = coef_a[0:1] * ref_a[0, part, :] + coef_b[0:1] * ref_b[0, part, :]
        for j in range(1, NB):
            acc = acc + (coef_a[j:j + 1] * ref_a[j, part, :] + coef_b[j:j + 1] * ref_b[j, part, :])
        return acc

    def spread(s):
        row = jnp.broadcast_to(column_s[s:s + 1, :], (8, LANES))
        return [jnp.broadcast_to(lane_sum(jnp.where(lane8 == sub8 + 8 * g, row, 0.0)), (8, LANES))
                for g in range(groups)]

    def y_finish(i, c, accs):
        lo, n = ych[c]
        for j in range(n):
            t = 8 + lo + j
            ybuf[i, me_p, t:t + 1, :] = jnp.sum(accs[j] + accs[n + j], axis=0, keepdims=True)
        y_send(i, c)

    def y_block(s, c, accs):
        lo, n = ych[c]
        accs = list(accs)
        for g in range(BLOCKS * groups):
            r = pl.ds(pl.multiple_of(s * (BLOCKS * LANES) + 8 * g, 8), 8)
            v = vb[r, :]
            for j in range(n):
                m = (g % 2) * n + j
                accs[m] = accs[m] + v * a[r, (lo + j) * LANES:(lo + j + 1) * LANES]
        return tuple(accs)

    def put(out, base, i, ref):
        for s in range(ref.shape[1]):
            part = slice(s * LANES, (s + 1) * LANES)
            row = jnp.broadcast_to(ref[i, s:s + 1, :], (NB, LANES))
            out[base:base + NB, part] = jnp.where(sub8 == i, row, out[base:base + NB, part])

    @pl.loop(0, NB)
    def _(i):
        masked = jnp.where(row_gl >= i, column_s[...], 0.0)
        unit_r = (row_gl == i).astype(jnp.float32)
        column_s[...] = masked

        @pl.when(i == 0)
        def _():
            a_cps[0].wait()

        ybuf[i, me_p, 7:8, :] = scalar_row(v_s, x_s, masked, me_p == 0, i)
        lo, n = ych[0]
        accs = [jnp.zeros((8, LANES), jnp.float32)] * (2 * n)
        for s in range(rs):
            for g, v in enumerate(spread(s)):
                r = pl.ds(s * LANES + 8 * g, 8)
                vb[r, :] = v
                for j in range(n):
                    m = (g % 2) * n + j
                    accs[m] = accs[m] + v * a[r, (lo + j) * LANES:(lo + j + 1) * LANES]
        for c in range(1, len(ych)):
            @pl.when(i == 0)
            def _(c=c):
                a_cps[c].wait()

            y_finish(i, c - 1, accs)
            zeros = (jnp.zeros((8, LANES), jnp.float32),) * (2 * ych[c][1])
            accs = lax.fori_loop(1, rs // BLOCKS, functools.partial(lambda s, t, c: y_block(s, c, t), c=c),
                                 y_block(0, c, zeros))
        y_finish(i, len(ych) - 1, accs)

        @pl.when(me_p != 0)
        def _():
            row_copy(i, 1).wait_recv()

        for c, (lo, n) in enumerate(ych):
            y_wait(i, c, y_rsem.at[lax.rem(i, 2), c])
            if c == 0:
                v_coef, x_coef, v_at, x_at, misc = unpack(ybuf.at[i], np_)
                beta, tau, denom = householder(misc[0:1], misc[1:2])
                inv = 1.0 / denom
                v_s[i] = (masked - beta * unit_r) * inv
                scal_o[0, pl.ds(i, 1), :] = beta
                scal_o[2, pl.ds(i, 1), :] = tau
            part, buf = pl.ds(lo, n), pl.ds(8 + lo, n)
            summed = ybuf[i, 0, buf, :]
            for p in range(1, np_):
                summed = summed + ybuf[i, p, buf, :]
            row_eff = rowp[i, part, :] - combine(v_at, y_s, x_at, u_s, lo, n)
            trans = (summed - combine(v_coef, y_s, x_coef, u_s, lo, n) - beta * row_eff) * inv
            mine = col_gl(lo, n) > i
            y_new = jnp.where(mine, tau * trans, 0.0)
            y_s[i, part, :] = y_new
            ub[part, :] = jnp.where(mine, row_eff - y_new, 0.0)
            us = [jnp.broadcast_to(ub[lo + j:lo + j + 1, :], (8, LANES)) for j in range(n)]

            def product(r, us=us, lo=lo, n=n):
                p = [us[k] * a[r, (lo + k) * LANES:(lo + k + 1) * LANES] for k in range(2)]
                for j in range(2, n):
                    p[j % 2] = p[j % 2] + us[j] * a[r, (lo + j) * LANES:(lo + j + 1) * LANES]
                return p[0] + p[1]

            if c < len(ych) - 1:
                @pl.loop(0, rs // BLOCKS)
                def _(s, c=c, product=product):
                    for g in range(BLOCKS * groups):
                        r = pl.ds(pl.multiple_of(s * (BLOCKS * LANES) + 8 * g, 8), 8)
                        acc_s[r, :] = product(r) if c == 0 else acc_s[r, :] + product(r)
            else:
                row_m = ub[...]
                xbuf[i, me_q, 7:8, :] = scalar_row(y_s, u_s, row_m, me_q == 0, i + 1)
                for s in range(rs):
                    tile = jnp.zeros((8, LANES), jnp.float32)
                    for g in range(groups):
                        r = pl.ds(s * LANES + 8 * g, 8)
                        tile = jnp.where(lane8 == sub8 + 8 * g, lane_sum(acc_s[r, :] + product(r)), tile)
                    xbuf[i, me_q, 8 + s:9 + s, :] = jnp.sum(tile, axis=0, keepdims=True)
                x_send(i)

        @pl.when(jnp.logical_and(me_p == 0, i < NB - 2))
        def _():
            for d in range(1, np_):
                row_copy(i + 2, d).start()

        @pl.when(jnp.logical_and(me_q != 0, i == 0))
        def _():
            col_copy(1, 1).wait_recv()

        for c in range(len(ych)):
            y_wait(i, c, y_ssem.at[c])
        put(left_o, 0, i, v_s)
        put(right_o, 0, i, y_s)

        @pl.when(i > 0)
        def _():
            put(left_o, NB, i - 1, x_s)
            put(right_o, NB, i - 1, u_s)

        unit_c = (col_gl(0, cs) == i + 1).astype(jnp.float32)
        x_wait(i, x_ssem)
        x_wait(i, x_rsem.at[lax.rem(i, 2)])
        y_coef, u_coef, y_at, u_at, misc2 = unpack(xbuf.at[i], nq)
        xsum = xbuf[i, 0, 8:8 + rs, :]
        for q in range(1, nq):
            xsum = xsum + xbuf[i, q, 8:8 + rs, :]
        beta2, tau2, denom2 = householder(misc2[0:1], misc2[1:2])
        col_next = colp[i + 1] - combine(y_at, v_s, u_at, x_s, 0, rs)
        inv2 = 1.0 / denom2
        prod = (xsum - combine(y_coef, v_s, u_coef, x_s, 0, rs) - beta2 * col_next) * inv2
        x_new = jnp.where(row_gl > i, tau2 * prod, 0.0)
        x_s[i] = x_new
        u_s[i] = (row_m - beta2 * unit_c) * inv2
        scal_o[1, pl.ds(i, 1), :] = beta2
        scal_o[3, pl.ds(i, 1), :] = tau2
        column_s[...] = col_next - x_new

    put(left_o, NB, NB - 1, x_s)
    put(right_o, NB, NB - 1, u_s)

    @pl.when(me_q == 0)
    def _():
        for h in range(2):
            for d in range(1, nq):
                col_copy(h, d).wait_send()

    @pl.when(me_p == 0)
    def _():
        @pl.loop(0, NB)
        def _(i):
            for d in range(1, np_):
                row_copy(i, d).wait_send()


def reduce_panel(matrix, np_, nq):
    rows, cols = matrix.shape
    rs, cs = rows // LANES, cols // LANES
    f32 = jnp.float32
    vmem = pl.BlockSpec(memory_space=pltpu.VMEM)
    dma = pltpu.SemaphoreType.DMA
    yc = len(Y_PARTS)
    return pl.pallas_call(
        functools.partial(panel_kernel, np_, nq),
        out_shape=(pltpu.VMEM((rows, cols), f32),
                   pltpu.VMEM((2 * NB, rows), f32),
                   pltpu.VMEM((2 * NB, cols), f32),
                   pltpu.VMEM((4, NB, LANES), f32)),
        in_specs=[pl.BlockSpec(memory_space=pl.ANY)],
        out_specs=(vmem, vmem, vmem, vmem),
        scratch_shapes=[
            pltpu.VMEM((rows, LANES), f32),
            pltpu.VMEM((NB, cols), f32),
            pltpu.VMEM((NB + 1, rs, LANES), f32),
            pltpu.VMEM((NB, cs, LANES), f32),
            pltpu.VMEM((NB, rs, LANES), f32),
            pltpu.VMEM((NB, rs, LANES), f32),
            pltpu.VMEM((NB, cs, LANES), f32),
            pltpu.VMEM((NB, cs, LANES), f32),
            pltpu.VMEM((rows, LANES), f32),
            pltpu.VMEM((cs, LANES), f32),
            pltpu.VMEM((rows, LANES), f32),
            pltpu.VMEM((NB, np_, 8 + cs, LANES), f32),
            pltpu.VMEM((NB, nq, 8 + rs, LANES), f32),
            pltpu.VMEM((rs, LANES), f32),
            dma((yc,)), dma, dma,
            dma((2, nq)), dma((2,)), dma((NB, np_)), dma((NB,)),
            dma((yc,)), dma((2, yc)), dma, dma((2,)),
        ],
        compiler_params=pltpu.CompilerParams(
            collective_id=0, has_side_effects=True, vmem_limit_bytes=20 * 1024 * 1024),
    )(matrix)


def pieces(x):
    hi = x.astype(jnp.bfloat16)
    rest = x - hi.astype(jnp.float32)
    mid = rest.astype(jnp.bfloat16)
    lo = (rest - mid.astype(jnp.float32)).astype(jnp.bfloat16)
    return hi, mid, lo


def update_kernel(a_ref, left_ref, right_ref, scal_ref, out_ref, coef_ref, left_p, right_p, slots, sems):
    me_p = lax.axis_index("prow")
    me_q = lax.axis_index("pcol")
    rows, cols = a_ref.shape
    depth, block = slots.shape[0], slots.shape[1]
    steps = rows // block
    dims = (((0,), (0,)), ((), ()))

    lh, lm, ll = pieces(left_ref[...])
    rh, rm, rl = pieces(right_ref[...])
    for k, (lp, rp) in enumerate(((lh, rh), (lh, rm), (lh, rl), (lm, rh), (lm, rm), (ll, rh))):
        left_p[2 * NB * k:2 * NB * (k + 1), :] = lp
        right_p[2 * NB * k:2 * NB * (k + 1), :] = rp
    lane = lax.broadcasted_iota(jnp.int32, (NB, LANES), 1)
    sub = lax.broadcasted_iota(jnp.int32, (NB, LANES), 0)
    for t in range(2):
        row = jnp.sum(jnp.where(lane == sub, scal_ref[2 + t], 0.0), axis=0, keepdims=True)
        coef_ref[t:t + 1, :] = row[:, 0:NB]

    def out_copy(step):
        slot = lax.rem(step, depth)
        part = pl.ds(pl.multiple_of(step * block, block), block)
        return pltpu.make_async_copy(slots.at[slot], out_ref.at[part, :], sems.at[slot])

    @pl.loop(0, steps)
    def _(step):
        slot = lax.rem(step, depth)
        part = pl.ds(pl.multiple_of(step * block, block), block)

        @pl.when(step >= depth)
        def _():
            out_copy(step - depth).wait()

        left = left_p[:, part]
        slots[slot] = a_ref[part, :] - lax.dot_general(
            left, right_p[...], dims, preferred_element_type=jnp.float32)
        k = left.shape[0]
        src = lax.broadcasted_iota(jnp.int32, (k, LANES), 0)
        lane = lax.broadcasted_iota(jnp.int32, (k, LANES), 1)
        pick = jnp.logical_and(
            lane < NB, (src == lane) | (src == lane + 6 * NB) | (src == lane + 10 * NB))
        vt = lax.dot_general(left, jnp.where(pick, 1.0, 0.0).astype(jnp.bfloat16), dims,
                             preferred_element_type=jnp.float32)
        stored = jnp.logical_and(me_q == 0, lax.broadcasted_iota(jnp.int32, (block, LANES), 1) < NB)
        slots[slot, :, 0:LANES] = jnp.where(stored, vt, slots[slot, :, 0:LANES])

        @pl.when(jnp.logical_and(me_p == 0, step == 0))
        def _():
            vt = slots[0, 0:NB, 0:LANES]
            slots[0, 0:NB, :] = right_ref[NB:, :]

            @pl.when(me_q == 0)
            def _():
                r = lax.broadcasted_iota(jnp.int32, (NB, LANES), 0)
                c = lax.broadcasted_iota(jnp.int32, (NB, LANES), 1)
                slots[0, 0:NB, 0:LANES] = jnp.where(
                    c < r, vt,
                    jnp.where(c == r, scal_ref[0], jnp.where(c == r + 1, scal_ref[1], right_ref[NB:, 0:LANES])))

        out_copy(step).start()

    @pl.loop(max(0, steps - depth), steps)
    def _(step):
        out_copy(step).wait()


def apply_panel(matrix, left, right, scal):
    rows, cols = matrix.shape
    block = min(rows, UPDATE_ROWS)
    depth = min(UPDATE_SLOTS, rows // block)
    vmem = pl.BlockSpec(memory_space=pltpu.VMEM)
    return pl.pallas_call(
        update_kernel,
        out_shape=(jax.ShapeDtypeStruct((rows, cols), jnp.float32),
                   jax.ShapeDtypeStruct((2, NB), jnp.float32)),
        in_specs=[vmem, vmem, vmem, vmem],
        out_specs=(pl.BlockSpec(memory_space=pl.ANY), vmem),
        scratch_shapes=[pltpu.VMEM((12 * NB, rows), jnp.bfloat16),
                        pltpu.VMEM((12 * NB, cols), jnp.bfloat16),
                        pltpu.VMEM((depth, block, cols), jnp.float32),
                        pltpu.SemaphoreType.DMA((depth,))],
        compiler_params=pltpu.CompilerParams(vmem_limit_bytes=20 * 1024 * 1024),
    )(matrix, left, right, scal)


def solution(mesh):
    np_, nq = mesh.shape["prow"], mesh.shape["pcol"]

    def per_device(matrix):
        return apply_panel(*reduce_panel(matrix, np_, nq))

    return jax.shard_map(
        per_device, mesh=mesh, in_specs=(P("prow", "pcol"),),
        out_specs=(P("prow", "pcol"), P()), check_vma=False)
```

time: 123 us -> 109 us (0.89)
  Pallas kernels: 122 us -> 108 us
    pallas_call x1, Pallas kernels: 106 us -> 96 us  [reduce_panel(): pl.pallas_call(functools.partial(panel_kernel, np_, nq), out_shape=(pltpu...]
    pallas_call x1, Pallas kernels: 16.2 us -> 12.1 us  [apply_panel(): pl.pallas_call(update_kernel, out_shape=(jax.ShapeDtypeStruct((rows, cols...]
where the time goes in v2:
time: 109 us
  Pallas kernels  108 us (99%)
    pallas_call x1, Pallas kernels, reduce_panel(): pl.pallas_call(functools.partial(panel_kernel, np_, nq), out_shape=(pltpu...  96 us
    pallas_call x1, Pallas kernels, apply_panel(): pl.pallas_call(update_kernel, out_shape=(jax.ShapeDtypeStruct((rows, cols...  12.1 us

profile of v2, /device:TPU:0, one launch (start us, length us, event | category | flops | bytes accessed | tf_op | source)
XLA Modules:
  0.0 108.7 jit_solution(2834804266954065377)
XLA Ops:
  0.6 96.0 %shard_map.30 = (f32[2048,4096]{1,0:T(8,128)S(1)}, f32[16,2048]{1,0:T(8,128)S(1)}, f32[16,4096]{1,0:T(8,128)S(1)}, f32[4,8,128]{2,1,0:T(8,128)S(1)}) custom-call(f32[2048,4096]{1,0:T(8,128)} %a_hbm.1), custom_call_target="tpu_custom_call" | custom-call | tf_op jit(solution)/shard_map/pallas_call | solution.py:361
  96.6 12.1 %shard_map.31 = (f32[2048,4096]{1,0:T(8,128)}, f32[2,8]{1,0:T(2,128)}) custom-call(f32[2048,4096]{1,0:T(8,128)S(1)} %get-tuple-element.6.a_ref, f32[16,2048]{1,0:T(8,128)S(1)} %get-tuple-element.7.left_ref, f32[16,4096]{1,0:T(8,128)S(1)} %get-tuple-element.8.right_ref, f32[4,8,128]{2,1,0:T(8,128)S(1)} %get-tuple-element.9.scal_ref), custom_call_target="tpu_custom_call" | custom-call | tf_op jit(solution)/shard_map/pallas_call | solution.py:472

commit v3 on v2

--- a/solution.py
+++ b/solution.py
@@ -13,7 +13,7 @@
 Y_PARTS = (1, 2, 2, 2, 1)
 UPDATE_ROWS = 128
 UPDATE_SLOTS = 6
-BLOCKS = 2
+BLOCKS = 4
 MESH = pl.DeviceIdType.MESH
 
 

time: 109 us -> 108 us (level)
  no operation moved by 1% of the time
where the time goes in v3:
time: 108 us
  Pallas kernels  108 us (100%)
    pallas_call x1, Pallas kernels, reduce_panel(): pl.pallas_call(functools.partial(panel_kernel, np_, nq), out_shape=(pltpu...  95.5 us
    pallas_call x1, Pallas kernels, apply_panel(): pl.pallas_call(update_kernel, out_shape=(jax.ShapeDtypeStruct((rows, cols...  12.1 us

profile of v3, /device:TPU:0, one launch (start us, length us, event | category | flops | bytes accessed | tf_op | source)
XLA Modules:
  0.0 108.3 jit_solution(16608296334383664271)
XLA Ops:
  0.6 95.5 %shard_map.30 = (f32[2048,4096]{1,0:T(8,128)S(1)}, f32[16,2048]{1,0:T(8,128)S(1)}, f32[16,4096]{1,0:T(8,128)S(1)}, f32[4,8,128]{2,1,0:T(8,128)S(1)}) custom-call(f32[2048,4096]{1,0:T(8,128)} %a_hbm.1), custom_call_target="tpu_custom_call" | custom-call | tf_op jit(solution)/shard_map/pallas_call | solution.py:361
  96.2 12.1 %shard_map.31 = (f32[2048,4096]{1,0:T(8,128)}, f32[2,8]{1,0:T(2,128)}) custom-call(f32[2048,4096]{1,0:T(8,128)S(1)} %get-tuple-element.6.a_ref, f32[16,2048]{1,0:T(8,128)S(1)} %get-tuple-element.7.left_ref, f32[16,4096]{1,0:T(8,128)S(1)} %get-tuple-element.8.right_ref, f32[4,8,128]{2,1,0:T(8,128)S(1)} %get-tuple-element.9.scal_ref), custom_call_target="tpu_custom_call" | custom-call | tf_op jit(solution)/shard_map/pallas_call | solution.py:472
